TPU v7x, 256 devices: a whole 4x4x8 slice. The times are simulated.
256 devices in a mesh: bx: 16 (over x, y), by: 16 (over z, core).
Axes of the slice: x: 4, y: 4, z: 8, core: 2. Of those that a mesh axis runs over, the one named last changes fastest.
Arguments:
- forcing: float32 [2432, 4096], P('by', 'bx'), may hold values from -20 to 20
- guess: float32 [2432, 4096], P('by', 'bx'), may hold values from -3 to 3
- shift: float32 [2432, 4096], P('by', 'bx'), may hold values from 0.05 to 2
- ocean_mask: int32 [2432, 4096], P('by', 'bx'), may hold values 0 or 1
Outputs:
- solution_field: float32 [2432, 4096], P('by', 'bx')
- residual: float32 [2432, 4096], P('by', 'bx')
- residual_norm: float32 [], replicated
All inputs are finite; a program needn't handle non-finite values. No bound on the sum of `ocean_mask` on one device may be relied on, other than what follows from the above.
Results may differ from a plain program's by a relative error of at most 0.00002.
Values sent between devices are 32-bit elements; how exact they have to be, the bound alone decides.
A program may use at most 64 MiB of HBM per device.

v0:
```python
import jax
import jax.numpy as jnp
from jax import lax
from jax.sharding import PartitionSpec as P

ITERS = 4


LOW_BOUND = 0.05
HIGH_BOUND = 14.5


def padded_2(block, sides, width):
    for axis, dim in sides:
        count = lax.axis_size(axis)
        forward = [(i, i + 1) for i in range(count - 1)]
        forward.append((count - 1, 0))
        backward = [(target, source) for source, target in forward]
        low = lax.ppermute(
            lax.slice_in_dim(block, block.shape[dim] - width, None, axis=dim), axis, forward
        )
        high = lax.ppermute(lax.slice_in_dim(block, 0, width, axis=dim), axis, backward)
        block = jnp.concatenate([low, block, high], axis=dim)
    return block


def sent_to_all(x, axis):
    copies = jnp.broadcast_to(x, (lax.axis_size(axis), *x.shape))
    return lax.all_to_all(copies, axis, split_axis=0, concat_axis=0, tiled=True)


def laid_out(tiles, dim):
    tiles = jnp.moveaxis(tiles, 0, dim)
    dims = tiles.shape
    return tiles.reshape(*dims[:dim], dims[dim] * dims[dim + 1], *dims[dim + 2 :])


def gather_directly(x, axis, dim):
    tiles = sent_to_all(x, axis)
    return laid_out(tiles, dim)


def gather_turned(arrays, axis, dims):
    turned = [jnp.moveaxis(a, dim, 0) for a, dim in zip(arrays, dims)]
    both = jnp.concatenate([t.reshape(len(t), -1) for t in turned], axis=1)
    filled, at, outs = (lax.all_gather(both, axis, axis=0, tiled=True), 0, [])
    for t, dim in zip(turned, dims):
        piece = filled[:, at : at + t[0].size].reshape(-1, *t.shape[1:])
        outs.append(jnp.moveaxis(piece, 0, dim))
        at += t[0].size
    return tuple(outs)


def stencil_padded(padded, shift, mask_f):
    center = padded[1:-1, 1:-1]
    sides = padded[2:, 1:-1] + padded[:-2, 1:-1] + padded[1:-1, 2:] + padded[1:-1, :-2]
    corners = padded[2:, 2:] + padded[2:, :-2] + padded[:-2, 2:] + padded[:-2, :-2]
    return mask_f * ((6.0 + shift) * center - sides - 0.5 * corners)


def crop_cycle(values, cycle):
    return values[cycle : values.shape[0] - cycle, cycle : values.shape[1] - cycle]


def local_stencil(values, shift_full, mask_full):
    cycle = (shift_full.shape[0] - values.shape[0]) // 2 + 1
    return stencil_padded(values, crop_cycle(shift_full, cycle), crop_cycle(mask_full, cycle))


def deep_inputs(forcing, guess, shift, mask_f):
    rows, cols = forcing.shape
    depth = ITERS + 1
    stacked = jnp.stack([forcing, guess, shift, mask_f])
    padded = padded_2(stacked, (("bx", 2), ("by", 1)), depth)
    top_rows = stacked[:, rows - depth :, :]
    whole_top = gather_directly(top_rows, "bx", 2)
    flipped = whole_top[:, ::-1, ::-1]
    extended = jnp.concatenate([flipped[:, :, -depth:], flipped, flipped[:, :, :depth]], axis=2)
    ghost = lax.dynamic_slice_in_dim(extended, lax.axis_index("bx") * cols, cols + 2 * depth, 2)
    row_index = lax.axis_index("by")
    upper_rows = jnp.where(row_index == lax.axis_size("by") - 1, ghost, padded[:, rows + depth :])
    lower_rows = jnp.where(row_index == 0, jnp.zeros_like(ghost), padded[:, :depth])
    return jnp.concatenate([lower_rows, padded[:, depth : rows + depth], upper_rows], axis=1)


def pair_add(first, second):
    total = first[0] + second[0]
    backed = total - first[0]
    error = first[0] - (total - backed) + (second[0] - backed)
    error = error + first[1] + second[1]
    upper = total + error
    lower = error - (upper - total)
    return (upper, lower)


def tree_total(uppers, lowers):
    while uppers.shape[0] > 1:
        if uppers.shape[0] % 2 == 1:
            uppers = jnp.concatenate([uppers, jnp.zeros((1,), uppers.dtype)])
            lowers = jnp.concatenate([lowers, jnp.zeros((1,), lowers.dtype)])
        uppers, lowers = pair_add((uppers[0::2], lowers[0::2]), (uppers[1::2], lowers[1::2]))
    return (uppers[0], lowers[0])


def per_device(forcing, guess, shift, ocean_mask):
    mask_f = ocean_mask.astype(jnp.float32)
    theta = (HIGH_BOUND + LOW_BOUND) / 2.0
    delta = (HIGH_BOUND - LOW_BOUND) / 2.0
    sigma = theta / delta
    rho = 1.0 / sigma
    full = deep_inputs(forcing, guess, shift, mask_f)
    forcing_full = full[0]
    guess_full = full[1]
    shift_full = full[2]
    mask_full = full[3]
    iterate = mask_full * guess_full
    resid = crop_cycle(mask_full * forcing_full, 1) - local_stencil(iterate, shift_full, mask_full)
    direction = resid / theta
    iterate = crop_cycle(iterate, 1)
    for sweep in range(ITERS):
        iterate = iterate + direction
        image = local_stencil(direction, shift_full, mask_full)
        resid = crop_cycle(resid, 1) - image
        rho_next = 1.0 / (2.0 * sigma - rho)
        direction = rho_next * rho * crop_cycle(direction, 1) + 2.0 * rho_next / delta * resid
        rho = rho_next
        iterate = crop_cycle(iterate, 1)
    row_sums = jnp.sum(resid * resid, axis=1)
    upper, lower = tree_total(row_sums, jnp.zeros_like(row_sums))
    all_upper, all_lower = gather_turned((upper[None], lower[None]), ("bx", "by"), (0, 0))
    upper, lower = tree_total(all_upper, all_lower)
    grid_cells = resid.shape[0] * lax.axis_size("by") * resid.shape[1] * lax.axis_size("bx")
    norm_value = jnp.sqrt((upper + lower) / grid_cells)
    return (iterate, resid, norm_value)


def solution(mesh):
    in_specs = (P("by", "bx"), P("by", "bx"), P("by", "bx"), P("by", "bx"))
    out_specs = (P("by", "bx"), P("by", "bx"), P())
    return jax.shard_map(
        per_device, mesh=mesh, in_specs=in_specs, out_specs=out_specs, check_vma=False
    )
```

profile of v0, /device:TPU:1, one launch (start us, length us, event | category | flops | bytes accessed | tf_op | source)
XLA Modules:
  0.0 117.5 jit_solution(8575989142189107592)
XLA Ops:
  0.6 1.1 stack.15
  1.8 0.8 copy-done.1
  2.7 0.8 copy-done.2
  3.7 0.6 pad_maximum_fusion.1
  4.3 0.2 fusion.39
  4.5 2.2 %collective-permute-start = (f32[4,152,5]{2,0,1:T(4,128)S(1)}, f32[4,152,5]{2,0,1:T(4,128)S(1)}, u32[]{:S(2)}, u32[]{:S(2)}) collective-permute-start(f32[4,152,5]{2,0,1:T(4,128)S(1)} %get-tuple-element.75), channel_id=1, source_target_pairs={{0,16},{16,32},{32,48},{48,64},{64,80},{80,96},{96,112},{112,128},... | collective-permute-start | bytes 36488 | tf_op jit(solution)/shard_map/ppermute | solution.py:19
  6.7 3.7 %collective-permute-start.1 = (f32[4,152,5]{2,0,1:T(4,128)S(1)}, f32[4,152,5]{2,0,1:T(4,128)S(1)}, u32[]{:S(2)}, u32[]{:S(2)}) collective-permute-start(f32[4,152,5]{2,0,1:T(4,128)S(1)} %get-tuple-element.76), channel_id=1, source_target_pairs={{16,0},{32,16},{48,32},{64,48},{80,64},{96,80},{112,96},{128,112},... | collective-permute-start | bytes 36488 | tf_op jit(solution)/shard_map/ppermute | solution.py:22
  10.4 0.8 broadcast_in_dim.7
  11.2 3.5 %all-to-all-start = ((f32[16,4,5,256]{3,1,2,0:T(4,128)}), f32[16,4,5,256]{3,1,2,0:T(4,128)S(1)}, u32[]{:S(2)}, u32[]{:S(2)}) async-start(f32[16,4,5,256]{3,1,2,0:T(4,128)} %broadcast_in_dim.7), calls=%async_computation | async-start | bytes 655360 | tf_op jit(solution)/shard_map/all_to_all | solution.py:29
  14.8 0.8 collective-permute-done
  15.5 0.2 pad_maximum_fusion.7
  15.8 6.2 %collective-permute-start.2 = (f32[4,5,266]{2,0,1:T(4,128)S(1)}, f32[4,5,266]{2,0,1:T(4,128)S(1)}, u32[]{:S(2)}, u32[]{:S(2)}) collective-permute-start(f32[4,5,266]{2,0,1:T(4,128)S(1)} %get-tuple-element.69), channel_id=1, source_target_pairs={{0,1},{1,2},{2,3},{3,4},{4,5},{5,6},{6,7},{7,8},{8,9},{9,10},{10,1... | collective-permute-start | bytes 63848 | tf_op jit(solution)/shard_map/ppermute | solution.py:19
  22.0 1.0 collective-permute-done.2
  23.1 3.1 %rev.3 = f32[4,5,4096]{2,0,1:T(4,128)S(1)} reverse(f32[4,5,4096]{2,0,1:T(4,128)S(1)} %bitcast.28), dimensions={1,2} | reverse | bytes 655360 | tf_op jit(solution)/shard_map/rev | solution.py:77
  26.3 0.4 concatenate.31
  26.9 2.3 %pad_maximum_fusion = f32[4,162,266]{2,0,1:T(4,128)S(1)} fusion(f32[4,5,266]{2,0,1:T(4,128)S(1)} %dynamic-slice_select_fusion, f32[4,152,5]{2,0,1:T(4,128)S(1)} %collective-permute-done.1, f32[1,152,256]{2,0,1:T(1,128)S(1)} %stack.18, f32[1,152,256]{2,0,1:T(1,128)S(1)} %stack.17, f32[1,152,256]{2,0,1:T(1,128)S(1)} %stack.16, f32[1,152,256]{2,0,1:T(1,128)S(1)} %stack.15, ...), kind=kLoop, calls=%fused_computation | loop fusion | flops 1206576 | bytes 1378944 | tf_op jit(solution)/shard_map/concatenate | solution.py:83
  29.2 0.7 fusion.38
  30.2 0.7 broadcast_multiply_fusion
  31.0 0.6 multiply_add_fusion.2
  31.8 0.6 multiply_add_fusion.1
  32.4 0.6 multiply_add_fusion
  33.1 1.4 %multiply_reduce_fusion = (f32[152]{0:T(256)S(1)}, f32[152,256]{1,0:T(8,128)}, f32[152,256]{1,0:T(8,128)}) fusion(f32[154,258]{1,0:T(8,128)S(1)} %get-tuple-element.61, f32[162,266]{1,0:T(8,128)S(1)} %bitcast.26, f32[162,266]{1,0:T(8,128)S(1)} %get-tuple-element.90, f32[154,258]{1,0:T(8,128)S(1)} %get-tuple-element.62, f32[154,258]{1,0:T(8,128)S(1)} %get-tuple-element.80, ...), kind=kLoop, calls=%fused_computation.80 | loop fusion | flops 739176 | bytes 2802272 | tf_op jit(solution)/shard_map/reduce_sum | solution.py:128
  38.0 0.6 fusion.44
  41.0 0.6 fusion.43
  43.5 63.3 %all-gather = f32[256,1,2]{2,1,0:T(1,128)S(1)} all-gather(f32[1,1,2]{2,1,0:T(1,128)S(1)} %maximum_bitcast_fusion), channel_id=1, replica_groups=mesh['bx'=16,'by'=16] {'bx','by'}, dimensions={0}, use_global_device_ids=true | all-gather | bytes 2056 | tf_op jit(solution)/shard_map/all_gather | solution.py:46
  106.8 0.2 slice_reduce_fusion
  107.1 0.2 slice.547
  107.3 0.2 slice.546
  107.5 0.2 slice.544
  107.7 0.2 slice.543
  110.9 0.6 fusion.42
  113.9 0.6 fusion.41
  (110 shorter events, 7.6 us)
Async XLA Ops:
  0.6 1.1 copy-start
  1.7 0.9 copy-start.1
  2.6 0.9 copy-start.2
  4.5 11.0 %collective-permute-start = (f32[4,152,5]{2,0,1:T(4,128)S(1)}, f32[4,152,5]{2,0,1:T(4,128)S(1)}, u32[]{:S(2)}, u32[]{:S(2)}) collective-permute-start(f32[4,152,5]{2,0,1:T(4,128)S(1)} %get-tuple-element.75), channel_id=1, source_target_pairs={{0,16},{16,32},{32,48},{48,64},{64,80},{80,96},{96,112},{112,128},... | collective-permute-start | bytes 36488 | tf_op jit(solution)/shard_map/ppermute | solution.py:19
  6.7 8.9 %collective-permute-start.1 = (f32[4,152,5]{2,0,1:T(4,128)S(1)}, f32[4,152,5]{2,0,1:T(4,128)S(1)}, u32[]{:S(2)}, u32[]{:S(2)}) collective-permute-start(f32[4,152,5]{2,0,1:T(4,128)S(1)} %get-tuple-element.76), channel_id=1, source_target_pairs={{16,0},{32,16},{48,32},{64,48},{80,64},{96,80},{112,96},{128,112},... | collective-permute-start | bytes 36488 | tf_op jit(solution)/shard_map/ppermute | solution.py:22
  11.2 11.7 %all-to-all-start = ((f32[16,4,5,256]{3,1,2,0:T(4,128)}), f32[16,4,5,256]{3,1,2,0:T(4,128)S(1)}, u32[]{:S(2)}, u32[]{:S(2)}) async-start(f32[16,4,5,256]{3,1,2,0:T(4,128)} %broadcast_in_dim.7), calls=%async_computation | async-start | bytes 655360 | tf_op jit(solution)/shard_map/all_to_all | solution.py:29
  15.8 7.2 %collective-permute-start.2 = (f32[4,5,266]{2,0,1:T(4,128)S(1)}, f32[4,5,266]{2,0,1:T(4,128)S(1)}, u32[]{:S(2)}, u32[]{:S(2)}) collective-permute-start(f32[4,5,266]{2,0,1:T(4,128)S(1)} %get-tuple-element.69), channel_id=1, source_target_pairs={{0,1},{1,2},{2,3},{3,4},{4,5},{5,6},{6,7},{7,8},{8,9},{9,10},{10,1... | collective-permute-start | bytes 63848 | tf_op jit(solution)/shard_map/ppermute | solution.py:19
  22.0 4.8 %collective-permute-start.3 = (f32[4,5,266]{2,0,1:T(4,128)S(1)}, f32[4,5,266]{2,0,1:T(4,128)S(1)}, u32[]{:S(2)}, u32[]{:S(2)}) collective-permute-start(f32[4,5,266]{2,0,1:T(4,128)S(1)} %get-tuple-element.70), channel_id=1, source_target_pairs={{1,0},{2,1},{3,2},{4,3},{5,4},{6,5},{7,6},{8,7},{9,8},{10,9},{11,1... | collective-permute-start | bytes 63848 | tf_op jit(solution)/shard_map/ppermute | solution.py:22
where the time goes:
time: 118 us
  blocking collectives  63.3 us (54%)
  local copies, waits for them, and re-layouts  17.9 us (15%)
  starting transfers between devices  15.7 us (13%)
  between operations  10.8 us (9%)
  other arithmetic  8.12 us (7%)
  waiting for transfers between devices  1.77 us (2%)
    all_gather x1, blocking collectives, gather_turned(): filled, at, outs = (lax.all_gather(both, axis, axis=0, tiled=True), 0, [])  63.3 us
    ppermute x2, starting transfers between devices, padded_2(): lax.ppermute(lax.slice_in_dim(block, block.shape[dim] - width, None, axis...  8.39 us
    ppermute x2, starting transfers between devices, padded_2(): lax.ppermute(lax.slice_in_dim(block, 0, width, axis=dim), axis, backward)  3.73 us
    all_to_all x1, starting transfers between devices, sent_to_all(): return lax.all_to_all(copies, axis, split_axis=0, concat_axis=0, tiled=True)  3.54 us
    rev x1, local copies, waits for them, and re-layouts, deep_inputs(): flipped = whole_top[:, ::-1, ::-1]  3.06 us
    slice x16, local copies, waits for them, and re-layouts, tree_total(): uppers[1::2]  2.87 us
    slice x15, local copies, waits for them, and re-layouts, tree_total(): lowers[1::2]  2.7 us
  transfers between devices with their start and end apart: 5, of which 2 were waited for; matrix products, arithmetic and copies ran while one was open for 4% of the time, Pallas kernels for 0%

commit v1 on v0

v1 whole, which is shorter than its diff:
```python
import functools

import jax
import jax.numpy as jnp
from jax import lax
from jax.experimental import pallas as pl
from jax.experimental.pallas import tpu as pltpu
from jax.sharding import PartitionSpec as P

ITERS = 4
LOW_BOUND = 0.05
HIGH_BOUND = 14.5
MESH = pl.DeviceIdType.MESH
F32 = jnp.float32
L = 128
S = 8
F, X, C, M = range(4)


def pair_add(first, second):
    total = first[0] + second[0]
    backed = total - first[0]
    error = first[0] - (total - backed) + (second[0] - backed)
    error = error + first[1] + second[1]
    upper = total + error
    lower = error - (upper - total)
    return (upper, lower)


def tree_total(pairs):
    while len(pairs) > 1:
        odd = pairs[len(pairs) & ~1 :]
        pairs = [pair_add(a, b) for a, b in zip(pairs[0::2], pairs[1::2])] + odd
    return pairs[0]


def lanes(shape):
    return lax.broadcasted_iota(jnp.int32, shape, len(shape) - 1)


def smooth(tiles):
    lane = lanes(tiles[0].shape)
    left = [pltpu.roll(t, 1, 1) for t in tiles]
    right = [pltpu.roll(t, L - 1, 1) for t in tiles]
    n = len(tiles)
    out = []
    for k, t in enumerate(tiles):
        west = jnp.where(lane == 0, left[k - 1], left[k])
        east = jnp.where(lane == L - 1, right[(k + 1) % n], right[k])
        out.append(t + 0.5 * (west + east))
    return out


def reversed_tile(tile):
    lane = lanes(tile.shape)
    row = lax.broadcasted_iota(jnp.int32, tile.shape, 0)
    for bit in (1, 2, 4, 8, 16, 32, 64):
        tile = jnp.where(lane & bit != 0, pltpu.roll(tile, bit, 1), pltpu.roll(tile, L - bit, 1))
    for bit in (1, 2, 4):
        tile = jnp.where(row & bit != 0, pltpu.roll(tile, bit, 0), pltpu.roll(tile, S - bit, 0))
    return tile


def kernel(nbx, nby, f_hbm, g_hbm, s_hbm, m_hbm, x_hbm, r_hbm, norm_ref,
           e, mi, g, xo, ro, pack, fold, foldpack, colr, corn, ra, rb,
           in_sem, hs_sem, hr_sem, as_sem, ar_sem, bs_sem, br_sem, out_sem):
    bx, by = lax.axis_index("bx"), lax.axis_index("by")
    top = nby - 1
    rows = mi.shape[1]
    full = rows + 2 * S
    nt = rows // S
    nv = pack.shape[1]
    is_top, is_low = by == top, by == 0

    def dev(dx, dy):
        return (lax.rem(bx + dx + nbx, nbx), by + dy)

    loads = []
    for i, src in ((3, m_hbm), (1, g_hbm), (0, f_hbm), (2, s_hbm)):
        for t in range(2):
            dst = mi.at[t] if i == M else e.at[i, t, pl.ds(S, rows)]
            loads.append(pltpu.make_async_copy(src.at[:, pl.ds(L * t, L)], dst, in_sem.at[2 * i + t]))
            loads[-1].start()

    barrier = pltpu.get_barrier_semaphore()
    for o in range(1, nby):
        pl.semaphore_signal(barrier, 1, device_id=(bx, lax.rem(by + o, nby)), device_id_type=MESH)
    for o in range(1, nbx):
        pl.semaphore_signal(barrier, 1, device_id=(lax.rem(bx + o, nbx), by), device_id_type=MESH)
    for dy, there in ((1, by < top), (-1, by > 0)):
        @pl.when(there)
        def _():
            for dx in (1, -1):
                pl.semaphore_signal(barrier, 1, device_id=dev(dx, dy), device_id_type=MESH)

    zero_row = jnp.zeros((S, L), F32)
    for b in range(2):
        for t in range(3):
            g[b, t, 0:S] = zero_row
            g[b, t, pl.ds(S + full, S)] = zero_row

    @pl.when(is_low)
    def _():
        for i in range(4):
            for t in range(3):
                e[i, t, 0:S] = zero_row

    for c in loads:
        c.wait()
    for t in range(2):
        e[M, t, pl.ds(S, rows)] = mi[t].astype(F32)

    slot = lanes((S, L)) // 8
    for v in range(nv):
        for side in range(2):
            acc = zero_row
            for k in range(16):
                t, a = 4 * v + k // 4, k % 4
                if t < nt:
                    tile = e[a, 1 - side, pl.ds(S + S * t, S)]
                    acc = jnp.where(slot == k, pltpu.roll(tile, (8 * k + 8 * (1 - side)) % L, 1), acc)
            pack[side, v] = acc

    @pl.when(is_top)
    def _():
        for side in range(2):
            acc = zero_row
            for a in range(4):
                tile = reversed_tile(e[a, side, pl.ds(rows, S)])
                fold[a, 1 - side] = tile
                acc = jnp.where(slot == a, pltpu.roll(tile, (8 * a + 8 * (1 - side)) % L, 1), acc)
            foldpack[side] = acc

    pl.semaphore_wait(barrier, nbx + nby - 2 + jnp.where(is_top, 0, 2) + jnp.where(is_low, 0, 2))

    def remote(src, dst, sent, got, target):
        return pltpu.make_async_remote_copy(
            src_ref=src, dst_ref=dst, send_sem=hs_sem.at[sent], recv_sem=hr_sem.at[got],
            device_id=target, device_id_type=MESH)

    def strip(row):
        return e.at[:, pl.ds(0, 2), pl.ds(row, S)]

    last = nv - 1
    self_left = lax.rem(nbx - bx, nbx)
    self_right = lax.rem(2 * nbx - 2 - bx, nbx)
    not_top, not_low = by < top, by > 0
    fold_left = jnp.logical_and(is_top, self_left != bx)
    fold_right = jnp.logical_and(is_top, self_right != bx)
    sends = [
        (not_top, remote(pack.at[0, last], corn.at[0], 4, 4, dev(1, 1))),
        (not_top, remote(pack.at[1, last], corn.at[1], 5, 5, dev(-1, 1))),
        (not_low, remote(pack.at[0, 0], corn.at[2], 6, 6, dev(1, -1))),
        (not_low, remote(pack.at[1, 0], corn.at[3], 7, 7, dev(-1, -1))),
        (fold_left, remote(foldpack.at[0], corn.at[2], 8, 6, (self_left, by))),
        (fold_right, remote(foldpack.at[1], corn.at[3], 9, 7, (self_right, by))),
        (None, remote(pack.at[0], colr.at[0], 0, 0, dev(1, 0))),
        (None, remote(pack.at[1], colr.at[1], 1, 1, dev(-1, 0))),
        (not_top, remote(strip(rows), strip(0), 2, 2, dev(0, 1))),
        (is_top, remote(fold, strip(S + rows), 10, 3, (nbx - 1 - bx, by))),
        (not_low, remote(strip(S), strip(S + rows), 3, 3, dev(0, -1))),
    ]
    near = (bx, by)
    receipts = [
        (None, remote(pack.at[0], colr.at[0], 0, 0, near)),
        (None, remote(pack.at[1], colr.at[1], 1, 1, near)),
        (not_low, remote(strip(rows), strip(0), 2, 2, near)),
        (None, remote(strip(S), strip(S + rows), 3, 3, near)),
        (not_low, remote(pack.at[0, last], corn.at[0], 4, 4, near)),
        (not_low, remote(pack.at[1, last], corn.at[1], 5, 5, near)),
        (jnp.logical_or(not_top, fold_left), remote(pack.at[0, 0], corn.at[2], 6, 6, near)),
        (jnp.logical_or(not_top, fold_right), remote(pack.at[1, 0], corn.at[3], 7, 7, near)),
    ]

    def each(items, act):
        for cond, copy in items:
            if cond is None:
                act(copy)
            else:
                pl.when(cond)(functools.partial(act, copy))

    each(sends, lambda c: c.start())
    for k, (mine, target) in enumerate(((fold_left, self_left), (fold_right, self_right))):
        @pl.when(jnp.logical_and(is_top, target == bx))
        def _():
            corn[2 + k] = foldpack[k]

    @pl.when(is_low)
    def _():
        corn[0] = zero_row
        corn[1] = zero_row

    each(receipts, lambda c: c.wait_recv())
    each(sends, lambda c: c.wait_send())

    lane = lanes((S, L))
    for v in range(nv):
        for k in range(16):
            t, a = 4 * v + k // 4, k % 4
            if t < nt:
                e[a, 2, pl.ds(S + S * t, S)] = jnp.where(
                    lane < L // 2, pltpu.roll(colr[1, v], (L - 8 * k) % L, 1), pltpu.roll(colr[0, v], (2 * L - 8 - 8 * k) % L, 1))
    for side, (row, first) in enumerate(((0, 4 * ((nt - 1) % 4)), (S + rows, 0))):
        for a in range(4):
            k = first + a
            e[a, 2, pl.ds(row, S)] = jnp.where(
                lane < L // 2, pltpu.roll(corn[2 * side + 1], (L - 8 * k) % L, 1),
                pltpu.roll(corn[2 * side], (2 * L - 8 - 8 * k) % L, 1))

    theta = (HIGH_BOUND + LOW_BOUND) / 2.0
    delta = (HIGH_BOUND - LOW_BOUND) / 2.0
    sigma = theta / delta
    rho = 1.0 / sigma
    tall = 56
    blocks = [(a, min(tall, full - a)) for a in range(0, full, tall)]

    def own(a, n, value):
        lo, hi = max(a, S), min(a + n, S + rows)
        return pl.ds(lo - S, hi - lo), value[lo - a : hi - a]

    def add_up(a, n, tiles, fresh=None):
        for t in range(2):
            where, part = own(a, n, tiles[t])
            base = own(a, n, fresh[t])[1] if fresh else xo[where, pl.ds(L * t, L)]
            xo[where, pl.ds(L * t, L)] = base + part

    for a, n in blocks:
        at = pl.ds(a, n)
        v = [e[M, t, at] * e[X, t, at] for t in range(3)]
        for t, h in enumerate(smooth(v)):
            g[0, t, pl.ds(S + a, n)] = h
            e[X, t, at] = v[t]

    for sweep in range(ITERS):
        now, later = sweep % 2, 1 - sweep % 2
        rho_next = 1.0 / (2.0 * sigma - rho)
        for a, n in blocks:
            at = pl.ds(a, n)
            fresh = []
            for t in range(3):
                mid = g[now, t, pl.ds(S + a, n)]
                tall_sum = (mid + mid) + (g[now, t, pl.ds(S + a - 1, n)] + g[now, t, pl.ds(S + a + 1, n)])
                m, v = e[M, t, at], e[X, t, at]
                if sweep == 0:
                    c = m * (8.0 + e[C, t, at])
                    e[C, t, at] = c
                    r = m * e[F, t, at] - (c * v - m * tall_sum)
                    d = r * (1.0 / theta)
                    if t < 2:
                        where, base = own(a, n, v)
                        xo[where, pl.ds(L * t, L)] = base + own(a, n, d)[1]
                else:
                    r = e[F, t, at] - (e[C, t, at] * v - m * tall_sum)
                    d = (rho_next * rho) * v + (2.0 * rho_next / delta) * r
                    if t < 2:
                        where, part = own(a, n, d)
                        xo[where, pl.ds(L * t, L)] = xo[where, pl.ds(L * t, L)] + part
                e[F, t, at] = r
                e[X, t, at] = d
                fresh.append(d)
            for t, h in enumerate(smooth(fresh)):
                g[later, t, pl.ds(S + a, n)] = h
        if sweep > 0:
            rho = rho_next

    now = ITERS % 2
    x_out = pltpu.make_async_copy(xo, x_hbm, out_sem.at[0])
    x_out.start()
    sums = []
    for a in range(S, S + rows, 4 * S):
        n = min(4 * S, S + rows - a)
        at = pl.ds(a, n)
        squares = []
        for t in range(2):
            mid = g[now, t, pl.ds(S + a, n)]
            tall_sum = (mid + mid) + (g[now, t, pl.ds(S + a - 1, n)] + g[now, t, pl.ds(S + a + 1, n)])
            r = e[F, t, at] - (e[C, t, at] * e[X, t, at] - e[M, t, at] * tall_sum)
            ro[pl.ds(a - S, n), pl.ds(L * t, L)] = r
            squares.append(r * r)
        row_sums = jnp.broadcast_to(jnp.sum(squares[0] + squares[1], axis=1, keepdims=True), (n, L))
        sums += [row_sums[k : k + S] for k in range(0, n, S)]
    r_out = pltpu.make_async_copy(ro, r_hbm, out_sem.at[1])
    r_out.start()

    pair = tree_total([(q, jnp.zeros_like(q)) for q in sums])
    for bit in (4, 2, 1):
        pair = pair_add(pair, tuple(pltpu.roll(p, bit, 0) for p in pair))
    pair = tuple(p[0:1] for p in pair)

    sent = []
    for buf, me, n, ssem, rsem, target in (
        (ra, by, nby, as_sem, ar_sem, lambda p: (bx, p)),
        (rb, bx, nbx, bs_sem, br_sem, lambda p: (p, by)),
    ):
        buf[me, 0] = pair[0]
        buf[me, 1] = pair[1]
        for o in range(1, n):
            c = pltpu.make_async_remote_copy(
                src_ref=buf.at[me], dst_ref=buf.at[me], send_sem=ssem.at[o], recv_sem=rsem.at[me],
                device_id=target(lax.rem(me + o, n)), device_id_type=MESH)
            c.start()
            sent.append(c)
        for o in range(1, n):
            p = lax.rem(me + o, n)
            pltpu.make_async_remote_copy(
                src_ref=buf.at[p], dst_ref=buf.at[p], send_sem=ssem.at[o], recv_sem=rsem.at[p],
                device_id=target(p), device_id_type=MESH).wait_recv()
        pair = tree_total([(buf[p, 0], buf[p, 1]) for p in range(n)])

    cells = (rows * nby) * (2 * L * nbx)
    norm_ref[...] = jnp.sqrt((pair[0] + pair[1]) / float(cells))
    for c in sent:
        c.wait_send()
    x_out.wait()
    r_out.wait()


def solution(mesh):
    nbx, nby = mesh.shape["bx"], mesh.shape["by"]

    def step(forcing, guess, shift, ocean_mask):
        rows, cols = forcing.shape
        full, nt = rows + 2 * S, rows // S
        nv = -(-nt // 4)
        dma = pltpu.SemaphoreType.DMA
        x, r, norm = pl.pallas_call(
            functools.partial(kernel, nbx, nby),
            out_shape=(
                jax.ShapeDtypeStruct((rows, cols), F32),
                jax.ShapeDtypeStruct((rows, cols), F32),
                jax.ShapeDtypeStruct((1, L), F32),
            ),
            in_specs=[pl.BlockSpec(memory_space=pl.ANY)] * 4,
            out_specs=(
                pl.BlockSpec(memory_space=pl.ANY),
                pl.BlockSpec(memory_space=pl.ANY),
                pl.BlockSpec(memory_space=pltpu.VMEM),
            ),
            scratch_shapes=[
                pltpu.VMEM((4, 3, full, L), F32),
                pltpu.VMEM((2, rows, L), jnp.int32),
                pltpu.VMEM((2, 3, full + 2 * S, L), F32),
                pltpu.VMEM((rows, cols), F32),
                pltpu.VMEM((rows, cols), F32),
                pltpu.VMEM((2, nv, S, L), F32),
                pltpu.VMEM((4, 2, S, L), F32),
                pltpu.VMEM((2, S, L), F32),
                pltpu.VMEM((2, nv, S, L), F32),
                pltpu.VMEM((4, S, L), F32),
                pltpu.VMEM((nby, 2, 1, L), F32),
                pltpu.VMEM((nbx, 2, 1, L), F32),
                dma((8,)), dma((11,)), dma((8,)),
                dma((nby,)), dma((nby,)), dma((nbx,)), dma((nbx,)),
                dma((2,)),
            ],
            compiler_params=pltpu.CompilerParams(collective_id=0, has_side_effects=True),
        )(forcing, guess, shift, ocean_mask)
        return x, r, norm[0, 0]

    spec = P("by", "bx")
    return jax.shard_map(
        step, mesh=mesh, in_specs=(spec, spec, spec, spec), out_specs=(spec, spec, P()), check_vma=False
    )
```

time: 118 us -> 32.1 us (0.27)
  blocking collectives: 63.3 us -> 0 us
  Pallas kernels: 0 us -> 27.8 us
  starting transfers between devices: 15.7 us -> 0 us
  local copies, waits for them, and re-layouts: 17.9 us -> 2.29 us
  between operations: 10.8 us -> 1.81 us
  other arithmetic: 8.12 us -> 0 us
  waiting for transfers between devices: 1.77 us -> 0 us
    all_gather x1 -> x0, blocking collectives: 63.3 us -> none  [gather_turned(): filled, at, outs = (lax.all_gather(both, axis, axis=0, tiled=True), 0, [])]
    pallas_call x0 -> x1, Pallas kernels: none -> 27.8 us  [step(): pl.pallas_call(functools.partial(kernel, nbx, nby), out_shape=(jax.ShapeD...]
    ppermute x4 -> x0, starting transfers between devices: 12.1 us -> none  [the longest x2 8.39 us: padded_2(): lax.ppermute(lax.slice_in_dim(block, block.shape[dim] - width, None, axis...]
    slice x67 -> x0, local copies, waits for them, and re-layouts: 10.6 us -> none  [the longest x16 2.87 us: tree_total(): uppers[1::2]]
    all_to_all x1 -> x0, starting transfers between devices: 3.54 us -> none  [sent_to_all(): return lax.all_to_all(copies, axis, split_axis=0, concat_axis=0, tiled=True)]
    rev x1 -> x0, local copies, waits for them, and re-layouts: 3.06 us -> none  [deep_inputs(): flipped = whole_top[:, ::-1, ::-1]]
    concatenate x7 -> x0, other arithmetic: 2.79 us -> none  [the longest x1 2.33 us: deep_inputs(): jnp.concatenate([lower_rows, padded[:, depth:rows + depth], upper_rows],...]
    add x17 -> x0, other arithmetic: 2.12 us -> none  [the longest x3 1.94 us: per_device(): rho_next * rho * crop_cycle(direction, 1) + 2.0 * rho_next / delta * resid]
  transfers between devices with their start and end apart: 5 -> 0, of which waited for: 2 -> 0; matrix products, arithmetic and copies ran while one was open for 4% -> 0% of each run, Pallas kernels for 0% -> 0%
where the time goes in v1:
time: 32.1 us; the launch traced here: 31.9 us
  Pallas kernels  27.8 us (87%)
  local copies, waits for them, and re-layouts  2.29 us (7%)
  between operations  1.81 us (6%)
    pallas_call x1, Pallas kernels, step(): pl.pallas_call(functools.partial(kernel, nbx, nby), out_shape=(jax.ShapeD...  27.8 us
    unnamed x6, local copies, waits for them, and re-layouts  2.29 us

profile of v1, /device:TPU:1, one launch (start us, length us, event | category | flops | bytes accessed | tf_op | source)
XLA Modules:
  0.0 31.9 jit_solution(11398207270730926268)
XLA Ops:
  0.6 27.8 %shard_map.67 = (f32[152,256]{1,0:T(8,128)}, f32[152,256]{1,0:T(8,128)}, f32[1,128]{1,0:T(1,128)}) custom-call(f32[152,256]{1,0:T(8,128)} %f_hbm.1, f32[152,256]{1,0:T(8,128)} %g_hbm.1, f32[152,256]{1,0:T(8,128)} %s_hbm.1, s32[152,256]{1,0:T(8,128)} %m_hbm.1), custom_call_target="tpu_custom_call" | custom-call | tf_op jit(solution)/shard_map/pallas_call | solution.py:326
  28.4 0.0 copy-start
  28.5 1.6 %copy.10 = f32[152,256]{1,0:T(8,128)} copy(f32[152,256]{1,0:T(8,128)} %get-tuple-element.12) | data formatting | bytes 311296
  30.1 0.0 copy-done
  30.1 0.0 copy-start.1
  30.1 0.7 %copy.11 = f32[152,256]{1,0:T(8,128)} copy(f32[152,256]{1,0:T(8,128)S(1)} %copy-done) | data formatting | bytes 311296
  30.7 0.0 copy-done.1
Async XLA Ops:
  28.4 1.6 %copy-start = (f32[152,256]{1,0:T(8,128)S(1)}, f32[152,256]{1,0:T(8,128)}, u32[]{:S(2)}) copy-start(f32[152,256]{1,0:T(8,128)} %get-tuple-element.13) | copy-start | bytes 466948
  30.1 0.7 %copy-start.1 = (f32[1,128]{1,0:T(1,128)S(1)}, f32[1,128]{1,0:T(1,128)}, u32[]{:S(2)}) copy-start(f32[1,128]{1,0:T(1,128)} %get-tuple-element.8) | copy-start | bytes 1540
